TPU v7x, 32 devices: a whole 2x2x4 slice. The times are simulated.
32 devices in a mesh: dp: 4 (over z), seq: 8 (over y, x, core).
Axes of the slice: x: 2, y: 2, z: 4, core: 2. Of those that a mesh axis runs over, the one named last changes fastest.
Arguments:
- queries: bfloat16 [4, 2048, 512], P('dp', 'seq'), may hold values from -0.890625 to 0.890625
- keys: bfloat16 [4, 2048, 512], P('dp', 'seq'), may hold values from -0.890625 to 0.890625
- values: bfloat16 [4, 2048, 512], P('dp', 'seq'), may hold values from -6 to 6
- level_weights: float32 [4, 6, 4, 2048], P('dp', None, None, 'seq'), may hold values from 0.25 to 4
- proj: bfloat16 [512, 2048], P(None, 'seq'), may hold values from -0.25 to 0.25
- out_grad: bfloat16 [4, 2048, 2048], P('dp', 'seq'), may hold values from -0.59765625 to 0.59765625
Outputs:
- attended_out: bfloat16 [4, 2048, 2048], P('dp', 'seq')
- grad_queries: bfloat16 [4, 2048, 512], P('dp', 'seq')
- grad_keys: bfloat16 [4, 2048, 512], P('dp', 'seq')
- grad_values: bfloat16 [4, 2048, 512], P('dp', 'seq')
- grad_levels: float32 [4, 6, 4, 2048], P('dp', None, None, 'seq')
- grad_proj: float32 [512, 2048], P(None, 'seq')
All inputs are finite; a program needn't handle non-finite values.
Results may differ from a plain program's by a relative error of at most 0.0064.
Values may be sent and summed in bfloat16 or wider, within the bound.
No kernel may reach another device: no remote copies, remote signals or barrier semaphores. Data moves between devices by JAX's collectives and lax.ppermute only.
A program may use at most 64 MiB of HBM per device.

v0:
```python
import jax
import jax.numpy as jnp
from jax import lax
from jax.sharding import PartitionSpec as P


def partner_2(value, axis, stride):
    mask = 2**stride
    pairs = [(source, source ^ mask) for source in range(lax.axis_size(axis))]
    return lax.ppermute(value, axis, pairs)


def level_table(length, stretch, local_bits):
    place = lax.iota(jnp.int32, length)
    blocks = place // stretch
    apart = jnp.bitwise_xor(blocks[:, None], blocks[None, :])
    table = jnp.zeros((length, length), jnp.int32)
    for bit in range(local_bits):
        table = table + (apart >= 1 << bit).astype(jnp.int32)
    causal = place[:, None] >= place[None, :]
    return (table, causal)


def local_weights(lam, table, causal, local_bits):
    weights = jnp.zeros((lam.shape[1], table.shape[0], table.shape[1]), jnp.float32)
    for level in range(local_bits + 1):
        weights = weights + jnp.where(table[None] == level, lam[level][:, :, None], jnp.float32(0))
    return jnp.where(causal[None], weights, jnp.float32(0))


def marked_bit(index, bit):
    return jnp.bitwise_and(jnp.right_shift(index, bit), 1).astype(jnp.float32)


def shards(queries, keys, values, level_weights, proj, out_grad):
    tokens_here = queries.shape[1]
    heads = level_weights.shape[2]
    levels = level_weights.shape[1]
    width = queries.shape[2]
    size = width // heads
    scale = size ** (-0.5)
    span_count = lax.axis_size("seq")
    dev_bits = span_count.bit_length() - 1
    local_bits = levels - 1 - dev_bits
    stretch = tokens_here >> local_bits
    index = lax.axis_index("seq")
    shape = (tokens_here, heads, size)
    query = queries[0].reshape(shape)
    key = keys[0].reshape(shape)
    value = values[0].reshape(shape)
    lam = level_weights[0]
    grad_out = out_grad[0]
    table, causal = level_table(tokens_here, stretch, local_bits)
    scores = jnp.einsum("thd,shd->hts", query, key, preferred_element_type=jnp.float32)
    weights = local_weights(lam, table, causal, local_bits)
    probs = (scale * weights * scores).astype(jnp.bfloat16)
    total = jnp.einsum("hts,shd->thd", probs, value, preferred_element_type=jnp.float32)
    totals = jnp.einsum("shi,shj->hij", key, value, preferred_element_type=jnp.float32)
    running = totals
    states = []
    for bit in range(dev_bits):
        partner = partner_2(running, "seq", bit)
        states.append((marked_bit(index, bit) * partner).astype(jnp.bfloat16))
        running = running + partner
    cross = jnp.zeros_like(total)
    mapped = []
    for bit in range(dev_bits):
        image = jnp.einsum("thi,hij->thj", query, states[bit], preferred_element_type=jnp.float32)
        mapped.append(image)
        cross = cross + lam[local_bits + 1 + bit].T[:, :, None] * image
    attended = (total + scale * cross).astype(jnp.bfloat16).reshape(tokens_here, width)
    full_proj = lax.all_gather(proj, "seq", axis=1, tiled=True)
    out = jnp.dot(attended, full_proj, preferred_element_type=jnp.float32).astype(jnp.bfloat16)
    grad_att = lax.dot_general(
        grad_out, full_proj, (((1,), (1,)), ((), ())), preferred_element_type=jnp.float32
    ).astype(jnp.bfloat16)
    grad_heads = grad_att.reshape(shape)
    dprob = jnp.einsum("thd,shd->hts", grad_heads, value, preferred_element_type=jnp.float32)
    product = jnp.where(causal[None], scale * scores * dprob, jnp.float32(0))
    grads = [
        jnp.sum(jnp.where(table[None] == level, product, jnp.float32(0)), axis=2)
        for level in range(local_bits + 1)
    ]
    dscore = (scale * weights * dprob).astype(jnp.bfloat16)
    grad_q = jnp.einsum("hts,shd->thd", dscore, key, preferred_element_type=jnp.float32)
    grad_k = jnp.einsum("hts,thd->shd", dscore, query, preferred_element_type=jnp.float32)
    grad_v = jnp.einsum("hts,thd->shd", probs, grad_heads, preferred_element_type=jnp.float32)
    updates = []
    for bit in range(dev_bits):
        grads.append(scale * jnp.sum(grad_heads.astype(jnp.float32) * mapped[bit], axis=2).T)
        weighted = (
            scale * lam[local_bits + 1 + bit].T[:, :, None] * grad_heads.astype(jnp.float32)
        ).astype(jnp.bfloat16)
        updates.append(
            jnp.einsum("thi,thj->hij", query, weighted, preferred_element_type=jnp.float32)
        )
        grad_q = grad_q + jnp.einsum(
            "thj,hij->thi", weighted, states[bit], preferred_element_type=jnp.float32
        )
    pending = [marked_bit(index, bit) * updates[bit] for bit in range(dev_bits)]
    carried = jnp.zeros_like(totals)
    for bit in range(dev_bits):
        sending = jnp.stack(pending[bit:])
        arrived = partner_2(sending, "seq", bit)
        carried = carried + (1.0 - marked_bit(index, bit)) * arrived[0]
        for later in range(bit + 1, dev_bits):
            pending[later] = pending[later] + arrived[later - bit]
    returned = carried.astype(jnp.bfloat16)
    grad_k = grad_k + jnp.einsum(
        "shj,hij->shi", value, returned, preferred_element_type=jnp.float32
    )
    grad_v = grad_v + jnp.einsum("shi,hij->shj", key, returned, preferred_element_type=jnp.float32)
    shard = lax.psum_scatter(
        lax.dot_general(
            grad_out, attended, (((0,), (0,)), ((), ())), preferred_element_type=jnp.float32
        ),
        "seq",
        scatter_dimension=0,
        tiled=True,
    )
    shard = lax.psum(shard, "dp")
    grad_levels = jnp.stack(grads)[None]
    return (
        out[None],
        grad_q.astype(jnp.bfloat16).reshape(1, tokens_here, width),
        grad_k.astype(jnp.bfloat16).reshape(1, tokens_here, width),
        grad_v.astype(jnp.bfloat16).reshape(1, tokens_here, width),
        grad_levels,
        shard.T,
    )


def solution(mesh):
    return jax.shard_map(
        shards,
        mesh=mesh,
        in_specs=(
            P("dp", "seq", None),
            P("dp", "seq", None),
            P("dp", "seq", None),
            P("dp", None, None, "seq"),
            P(None, "seq"),
            P("dp", "seq", None),
        ),
        out_specs=(
            P("dp", "seq", None),
            P("dp", "seq", None),
            P("dp", "seq", None),
            P("dp", "seq", None),
            P("dp", None, None, "seq"),
            P(None, "seq"),
        ),
        check_vma=False,
    )
```

profile of v0, /device:TPU:0, one launch (start us, length us, event | category | flops | bytes accessed | tf_op | source)
XLA Modules:
  0.0 157.5 jit_solution(11511535724584984246)
XLA Ops:
  8.0 1.0 reshape_squeeze.10
  9.2 1.1 reshape_squeeze.11
  11.8 0.9 fusion.29
  12.7 1.3 fusion.31
  14.0 2.6 %collective-permute-start.1 = (f32[4,128,128]{2,1,0:T(8,128)S(1)}, f32[4,128,128]{2,1,0:T(8,128)S(1)}, u32[]{:S(2)}, u32[]{:S(2)}) collective-permute-start(f32[4,128,128]{2,1,0:T(8,128)S(1)} %add.93), channel_id=1, source_target_pairs={{0,2},{1,3},{2,0},{3,1},{4,6},{5,7},{6,4},{7,5},{8,10},{9,11},{10,... | collective-permute-start | bytes 786440 | tf_op jit(solution)/shard_map/ppermute | solution.py:10
  17.4 8.0 %collective-permute-done.1 = f32[4,128,128]{2,1,0:T(8,128)S(1)} collective-permute-done((f32[4,128,128]{2,1,0:T(8,128)S(1)}, f32[4,128,128]{2,1,0:T(8,128)S(1)}, u32[]{:S(2)}, u32[]{:S(2)}) %collective-permute-start.1) | collective-permute-done | bytes 262176 | tf_op jit(solution)/shard_map/ppermute | solution.py:10
  26.1 1.4 collective-permute-start.2
  27.5 1.1 convolution_bitcast_fusion.9
  28.6 14.4 %all-gather.2.cloned.1.call-done = bf16[512,2048]{1,0:T(8,128)(2,1)} async-done(((bf16[512,256]{1,0:T(8,128)(2,1)}), bf16[512,2048]{1,0:T(8,128)(2,1)}) %all-gather.2.cloned.1.call-update) | async-done | bytes 2097168 | tf_op jit(solution)/shard_map/all_gather | solution.py:72
  42.9 3.0 %convolution_convert_fusion.1 = bf16[256,512]{1,0:T(8,128)(2,1)} fusion(bf16[512,2048]{1,0:T(8,128)(2,1)} %all-gather.2.cloned.1.call-done, bf16[1,256,2048]{2,1,0:T(8,128)(2,1)S(1)} %copy-done), kind=kOutput, calls=%fused_computation.21 | convolution fusion | flops 537001984 | bytes 3407872 | tf_op jit(solution)/shard_map/dot_general | solution.py:74
  46.0 1.1 copy.24
  47.2 1.5 fusion.18
  49.4 2.7 %convolution_bitcast_fusion = f32[2048,512]{0,1:T(8,128)} fusion(bf16[256,512]{0,1:T(8,128)(2,1)S(1)} %bitcast.163, bf16[1,256,2048]{2,1,0:T(8,128)(2,1)S(1)} %copy-done), kind=kOutput, calls=%fused_computation | convolution fusion | flops 536870912 | bytes 5505024 | tf_op jit(solution)/shard_map/dot_general | solution.py:114
  56.5 1.5 fusion.55
  58.1 1.5 collective-permute-start.4
  60.1 12.2 %collective-permute-done.4 = f32[2,4,128,128]{2,3,1,0:T(8,128)S(1)} collective-permute-done((f32[2,4,128,128]{2,3,1,0:T(8,128)S(1)}, f32[2,4,128,128]{2,3,1,0:T(8,128)S(1)}, u32[]{:S(2)}, u32[]{:S(2)}) %collective-permute-start.4) | collective-permute-done | bytes 524320 | tf_op jit(solution)/shard_map/ppermute | solution.py:10
  73.1 1.1 collective-permute-start.5
  75.7 3.3 %fusion = bf16[1,256,2048]{2,1,0:T(8,128)(2,1)} fusion(bf16[256,512]{0,1:T(8,128)(2,1)S(1)} %bitcast.164, bf16[512,2048]{1,0:T(8,128)(2,1)} %all-gather.2.cloned.1.call-done), kind=kOutput, calls=%fused_computation.2 | convolution fusion | flops 537395200 | bytes 3407872 | tf_op jit(solution)/shard_map/dot_general | solution.py:73
  79.1 29.1 %reduce-scatter.2.cloned.1.call-done = f32[256,512]{0,1:T(8,128)} async-done(((f32[2048,512]{0,1:T(8,128)}), f32[256,512]{0,1:T(8,128)}) %reduce-scatter.2.cloned.1.call-update) | async-done | bytes 524304 | tf_op jit(solution)/shard_map/reduce_scatter | solution.py:113
  108.2 1.1 fusion.45
  109.6 0.8 copy.42
  110.6 0.8 copy.43
  111.5 37.6 %all-reduce.2.cloned.1.call-done = f32[512,256]{1,0:T(8,128)} async-done(((f32[512,256]{1,0:T(8,128)}), f32[512,256]{1,0:T(8,128)}) %all-reduce.2.cloned.1.call-update) | async-done | bytes 524304 | tf_op jit(solution)/shard_map/psum | solution.py:121
  149.1 1.9 %copy.96 = f32[512,256]{1,0:T(8,128)} copy(f32[512,256]{1,0:T(8,128)} %all-reduce.2.cloned.1.call-done) | data formatting | bytes 1048576
  (103 shorter events, 12.4 us)
Async XLA Ops:
  7.2 35.8 %copy-start = (bf16[1,256,2048]{2,1,0:T(8,128)(2,1)S(1)}, bf16[1,256,2048]{2,1,0:T(8,128)(2,1)}, u32[]{:S(2)}) copy-start(bf16[1,256,2048]{2,1,0:T(8,128)(2,1)} %param.11) | copy-start | bytes 3145732
  7.2 3.9 %copy-start.12 = (bf16[1,256,512]{2,1,0:T(8,128)(2,1)S(1)}, bf16[1,256,512]{2,1,0:T(8,128)(2,1)}, u32[]{:S(2)}) copy-start(bf16[1,256,512]{2,1,0:T(8,128)(2,1)} %param.6) | copy-start | bytes 786436
  7.2 4.0 %copy-start.19 = (f32[1,6,4,256]{3,2,1,0:T(4,128)S(1)}, f32[1,6,4,256]{3,2,1,0:T(4,128)}, u32[]{:S(2)}) copy-start(f32[1,6,4,256]{3,2,1,0:T(4,128)} %param.9) | copy-start | bytes 73732
  7.2 35.7 %all-gather.2.cloned.1.call-start = ((), (), s32[]{:S(2)}) async-start(), calls=%async_computation.1 | async-start | bytes 2359296 | tf_op jit(solution)/shard_map/all_gather | solution.py:72
  7.9 100.2 %reduce-scatter.2.cloned.1.call-start = ((), (), s32[]{:S(2)}) async-start(), calls=%async_computation.2 | async-start | bytes 4718592 | tf_op jit(solution)/shard_map/reduce_scatter | solution.py:113
  10.5 3.4 %collective-permute-start = (f32[4,128,128]{2,1,0:T(8,128)S(1)}, f32[4,128,128]{2,1,0:T(8,128)S(1)}, u32[]{:S(2)}, u32[]{:S(2)}) collective-permute-start(f32[4,128,128]{2,1,0:T(8,128)S(1)} %fusion.43), channel_id=1, source_target_pairs={{0,1},{1,0},{2,3},{3,2},{4,5},{5,4},{6,7},{7,6},{8,9},{9,8},{10,11... | collective-permute-start | bytes 786440 | tf_op jit(solution)/shard_map/ppermute | solution.py:10
  14.0 11.4 %collective-permute-start.1 = (f32[4,128,128]{2,1,0:T(8,128)S(1)}, f32[4,128,128]{2,1,0:T(8,128)S(1)}, u32[]{:S(2)}, u32[]{:S(2)}) collective-permute-start(f32[4,128,128]{2,1,0:T(8,128)S(1)} %add.93), channel_id=1, source_target_pairs={{0,2},{1,3},{2,0},{3,1},{4,6},{5,7},{6,4},{7,5},{8,10},{9,11},{10,... | collective-permute-start | bytes 786440 | tf_op jit(solution)/shard_map/ppermute | solution.py:10
  26.1 21.0 %collective-permute-start.2 = (f32[4,128,128]{2,1,0:T(8,128)}, f32[4,128,128]{2,1,0:T(8,128)S(1)}, u32[]{:S(2)}, u32[]{:S(2)}) collective-permute-start(f32[4,128,128]{2,1,0:T(8,128)} %add.95), channel_id=1, source_target_pairs={{0,4},{1,5},{2,6},{3,7},{4,0},{5,1},{6,2},{7,3},{8,12},{9,13},{10,... | collective-permute-start | bytes 786440 | tf_op jit(solution)/shard_map/ppermute | solution.py:10
  47.1 1.6 %copy-start.1 = (f32[256,4,128]{0,2,1:T(8,128)S(1)}, f32[256,4,128]{0,2,1:T(8,128)}, u32[]{:S(2)}) copy-start(f32[256,4,128]{0,2,1:T(8,128)} %convolution_bitcast_fusion.9) | copy-start | bytes 1572868
  47.1 1.6 %copy-start.5 = (f32[4,256,256]{1,2,0:T(8,128)S(1)}, f32[4,256,256]{1,2,0:T(8,128)}, u32[]{:S(2)}) copy-start(f32[4,256,256]{1,2,0:T(8,128)} %fusion.31) | copy-start | bytes 3145732
  47.1 1.6 %copy-start.13 = (pred[256,256]{0,1:T(8,128)(4,1)S(1)}, pred[256,256]{0,1:T(8,128)(4,1)}, u32[]{:S(2)}) copy-start(pred[256,256]{0,1:T(8,128)(4,1)} %get-tuple-element.31) | copy-start | bytes 196612
  47.1 1.6 %copy-start.16 = (pred[256,256]{0,1:T(8,128)(4,1)S(1)}, pred[256,256]{0,1:T(8,128)(4,1)}, u32[]{:S(2)}) copy-start(pred[256,256]{0,1:T(8,128)(4,1)} %iota_compare_fusion) | copy-start | bytes 196612
  47.1 1.6 %copy-start.21 = (f32[4,256]{1,0:T(4,128)S(1)}, f32[4,256]{1,0:T(4,128)}, u32[]{:S(2)}) copy-start(f32[4,256]{1,0:T(4,128)} %get-tuple-element.25) | copy-start | bytes 12292
  47.1 1.6 %copy-start.23 = (f32[4,256]{1,0:T(4,128)S(1)}, f32[4,256]{1,0:T(4,128)}, u32[]{:S(2)}) copy-start(f32[4,256]{1,0:T(4,128)} %get-tuple-element.26) | copy-start | bytes 12292
  47.1 1.6 %copy-start.25 = (f32[256,4]{0,1:T(4,128)S(1)}, f32[256,4]{0,1:T(4,128)}, u32[]{:S(2)}) copy-start(f32[256,4]{0,1:T(4,128)} %get-tuple-element.24) | copy-start | bytes 12292
  52.1 1.8 %copy-start.14 = (pred[256,256]{0,1:T(8,128)(4,1)S(1)}, pred[256,256]{0,1:T(8,128)(4,1)}, u32[]{:S(2)}) copy-start(pred[256,256]{0,1:T(8,128)(4,1)} %get-tuple-element.31) | copy-start | bytes 196612
  52.1 1.8 %copy-start.17 = (pred[256,256]{0,1:T(8,128)(4,1)S(1)}, pred[256,256]{0,1:T(8,128)(4,1)}, u32[]{:S(2)}) copy-start(pred[256,256]{0,1:T(8,128)(4,1)} %iota_compare_fusion) | copy-start | bytes 196612
  52.1 96.9 %all-reduce.2.cloned.1.call-start = ((), (), s32[]{:S(2)}) async-start(), calls=%async_computation.3 | async-start | bytes 1048576 | tf_op jit(solution)/shard_map/psum | solution.py:121
  53.6 4.4 %collective-permute-start.3 = (f32[3,4,128,128]{2,3,1,0:T(8,128)S(1)}, f32[3,4,128,128]{2,3,1,0:T(8,128)S(1)}, u32[]{:S(2)}, u32[]{:S(2)}) collective-permute-start(f32[3,4,128,128]{2,3,1,0:T(8,128)S(1)} %pad_maximum_fusion), channel_id=1, source_target_pairs={{0,1},{1,0},{2,3},{3,2},{4,5},{5,4},{6,7},{7,6},{8,9},{9,8},{10,11... | collective-permute-start | bytes 2359304 | tf_op jit(solution)/shard_map/ppermute | solution.py:10
  58.0 14.2 %copy-start.2 = (f32[3,4,128,128]{2,3,1,0:T(8,128)}, f32[3,4,128,128]{2,3,1,0:T(8,128)S(1)}, u32[]{:S(2)}) copy-start(f32[3,4,128,128]{2,3,1,0:T(8,128)S(1)} %collective-permute-done.3) | copy-start | bytes 2359300
  58.1 14.1 %collective-permute-start.4 = (f32[2,4,128,128]{2,3,1,0:T(8,128)S(1)}, f32[2,4,128,128]{2,3,1,0:T(8,128)S(1)}, u32[]{:S(2)}, u32[]{:S(2)}) collective-permute-start(f32[2,4,128,128]{2,3,1,0:T(8,128)S(1)} %pad_maximum_fusion.1), channel_id=1, source_target_pairs={{0,2},{1,3},{2,0},{3,1},{4,6},{5,7},{6,4},{7,5},{8,10},{9,11},{10,... | collective-permute-start | bytes 1572872 | tf_op jit(solution)/shard_map/ppermute | solution.py:10
  73.1 35.0 %collective-permute-start.5 = (f32[1,4,128,128]{2,3,1,0:T(8,128)}, f32[1,4,128,128]{2,3,1,0:T(8,128)}, u32[]{:S(2)}, u32[]{:S(2)}) collective-permute-start(f32[1,4,128,128]{2,3,1,0:T(8,128)} %fusion.20), channel_id=1, source_target_pairs={{0,4},{1,5},{2,6},{3,7},{4,0},{5,1},{6,2},{7,3},{8,12},{9,13},{10,... | collective-permute-start | bytes 786440 | tf_op jit(solution)/shard_map/ppermute | solution.py:10
  75.7 32.5 %copy-start.11 = (f32[2,4,128,128]{2,3,1,0:T(8,128)S(1)}, f32[2,4,128,128]{2,3,1,0:T(8,128)}, u32[]{:S(2)}) copy-start(f32[2,4,128,128]{2,3,1,0:T(8,128)} %copy-done.10) | copy-start | bytes 1572868
  79.1 31.3 %copy-start.9 = (f32[4,128,256]{2,1,0:T(8,128)S(1)}, f32[4,128,256]{2,1,0:T(8,128)}, u32[]{:S(2)}) copy-start(f32[4,128,256]{2,1,0:T(8,128)} %fusion.55) | copy-start | bytes 1572868
  (14 other events, 16.6 us)
Sparse Core Ops, SparseCore 0:
  9.9 32.9 all-gather.1
  52.2 55.8 reduce-scatter.1
  110.5 38.5 all-reduce.1
where the time goes:
time: 158 us; the launch traced here: 157 us
  waiting for transfers between devices  102 us (65%)
  matrix products  19.2 us (12%)
  between operations  14.2 us (9%)
  local copies, waits for them, and re-layouts  10.2 us (6%)
  starting transfers between devices  7.56 us (5%)
  other arithmetic  4.34 us (3%)
    psum x1, waiting for transfers between devices, shards(): shard = lax.psum(shard, 'dp')  37.6 us
    reduce_scatter x1, waiting for transfers between devices, shards(): lax.psum_scatter(lax.dot_general(grad_out, attended, (((0,), (0,)), ((),...  29.1 us
    ppermute x6, waiting for transfers between devices, partner_2(): return lax.ppermute(value, axis, pairs)  20.1 us
    all_gather x1, waiting for transfers between devices, shards(): full_proj = lax.all_gather(proj, 'seq', axis=1, tiled=True)  14.4 us
    ppermute x6, starting transfers between devices, partner_2(): return lax.ppermute(value, axis, pairs)  7.44 us
    unnamed x65, local copies, waits for them, and re-layouts  6.16 us
    dot_general x1, matrix products, shards(): jnp.dot(attended, full_proj, preferred_element_type=jnp.float32)  3.35 us
  transfers between devices with their start and end apart: 9, of which 5 were waited for; matrix products, arithmetic and copies ran while one was open for 16% of the time, Pallas kernels for 0%

commit v1 on v0

--- a/solution.py
+++ b/solution.py
@@ -118,7 +118,7 @@
         scatter_dimension=0,
         tiled=True,
     )
-    shard = lax.psum(shard, "dp")
+    shard = jnp.sum(lax.all_gather(shard, axis_name="dp"), axis=0)
     grad_levels = jnp.stack(grads)[None]
     return (
         out[None],

time: 158 us -> 163 us (1.032)
  other arithmetic: 4.34 us -> 9.97 us
  waiting for transfers between devices: 102 us -> 97.1 us
  matrix products: 19.2 us -> 23.6 us
    psum x1 -> x0, waiting for transfers between devices: 37.6 us -> none  [shards(): shard = lax.psum(shard, 'dp')]
    reduce_scatter x1, waiting for transfers between devices: 29.1 us -> 45.5 us  [shards(): lax.psum_scatter(lax.dot_general(grad_out, attended, (((0,), (0,)), ((),...]
    all_gather x0 -> x1, waiting for transfers between devices: none -> 15.9 us  [shards(): shard = jnp.sum(lax.all_gather(shard, axis_name='dp'), axis=0)]
    another operation x4, other arithmetic: 0.96 us -> 3.95 us  [shards(): sending = jnp.stack(pending[bit:])]
    unnamed x65 -> x74, local copies, waits for them, and re-layouts: 6.16 us -> 3.35 us
    all_gather x0 -> x1, local copies, waits for them, and re-layouts: none -> 2.2 us  [shards(): shard = jnp.sum(lax.all_gather(shard, axis_name='dp'), axis=0)]
    reduce_sum x0 -> x1, other arithmetic: none -> 2.14 us  [shards(): shard = jnp.sum(lax.all_gather(shard, axis_name='dp'), axis=0)]
    dot_general x1, matrix products: 0.64 us -> 2.75 us  [shards(): jnp.einsum('hts,thd->shd', dscore, query, preferred_element_type=jnp.floa...]
  transfers between devices with their start and end apart: 9 -> 9, of which waited for: 5 -> 6; matrix products, arithmetic and copies ran while one was open for 16% -> 20% of each run, Pallas kernels for 0% -> 0%
where the time goes in v1:
time: 163 us; the launch traced here: 162 us
  waiting for transfers between devices  97.1 us (60%)
  matrix products  23.6 us (14%)
  between operations  14.2 us (9%)
  other arithmetic  9.97 us (6%)
  local copies, waits for them, and re-layouts  9.61 us (6%)
  starting transfers between devices  7.91 us (5%)
    reduce_scatter x1, waiting for transfers between devices, shards(): lax.psum_scatter(lax.dot_general(grad_out, attended, (((0,), (0,)), ((),...  45.5 us
    ppermute x6, waiting for transfers between devices, partner_2(): return lax.ppermute(value, axis, pairs)  20.6 us
    all_gather x1, waiting for transfers between devices, shards(): shard = jnp.sum(lax.all_gather(shard, axis_name='dp'), axis=0)  15.9 us
    all_gather x1, waiting for transfers between devices, shards(): full_proj = lax.all_gather(proj, 'seq', axis=1, tiled=True)  14.4 us
    ppermute x6, starting transfers between devices, partner_2(): return lax.ppermute(value, axis, pairs)  7.8 us
    another operation x4, other arithmetic, shards(): sending = jnp.stack(pending[bit:])  3.95 us
    dot_general x3, matrix products, shards(): jnp.einsum('thi,hij->thj', query, states[bit], preferred_element_type=jnp...  3.41 us
    dot_general x1, matrix products, shards(): jnp.dot(attended, full_proj, preferred_element_type=jnp.float32)  3.36 us
  transfers between devices with their start and end apart: 9, of which 6 were waited for; matrix products, arithmetic and copies ran while one was open for 20% of the time, Pallas kernels for 0%

profile of v1, /device:TPU:0, one launch (start us, length us, event | category | flops | bytes accessed | tf_op | source)
XLA Modules:
  0.0 162.4 jit_solution(8227577753078349684)
XLA Ops:
  9.2 1.1 reshape_squeeze.11
  12.6 1.3 fusion.31
  13.9 2.6 %collective-permute-start.1 = (f32[4,128,128]{2,1,0:T(8,128)S(1)}, f32[4,128,128]{2,1,0:T(8,128)S(1)}, u32[]{:S(2)}, u32[]{:S(2)}) collective-permute-start(f32[4,128,128]{2,1,0:T(8,128)S(1)} %add.91), channel_id=1, source_target_pairs={{0,2},{1,3},{2,0},{3,1},{4,6},{5,7},{6,4},{7,5},{8,10},{9,11},{10,... | collective-permute-start | bytes 786440 | tf_op jit(solution)/shard_map/ppermute | solution.py:10
  17.4 8.0 %collective-permute-done.1 = f32[4,128,128]{2,1,0:T(8,128)S(1)} collective-permute-done((f32[4,128,128]{2,1,0:T(8,128)S(1)}, f32[4,128,128]{2,1,0:T(8,128)S(1)}, u32[]{:S(2)}, u32[]{:S(2)}) %collective-permute-start.1) | collective-permute-done | bytes 262176 | tf_op jit(solution)/shard_map/ppermute | solution.py:10
  26.1 1.4 collective-permute-start.2
  28.5 14.4 %all-gather.4.cloned.1.call-done = bf16[512,2048]{1,0:T(8,128)(2,1)} async-done(((bf16[512,256]{1,0:T(8,128)(2,1)}), bf16[512,2048]{1,0:T(8,128)(2,1)}) %all-gather.4.cloned.1.call-update) | async-done | bytes 2097168 | tf_op jit(solution)/shard_map/all_gather | solution.py:72
  42.9 3.0 %convolution_convert_fusion.1 = bf16[256,512]{1,0:T(8,128)(2,1)} fusion(bf16[512,2048]{1,0:T(8,128)(2,1)} %all-gather.4.cloned.1.call-done, bf16[1,256,2048]{2,1,0:T(8,128)(2,1)S(1)} %copy-done), kind=kOutput, calls=%fused_computation.21 | convolution fusion | flops 537001984 | bytes 3407872 | tf_op jit(solution)/shard_map/dot_general | solution.py:74
  47.2 2.1 %fusion.18 = (f32[256,4]{0,1:T(4,128)S(1)}, f32[256,4]{0,1:T(4,128)S(1)}, f32[256,4]{0,1:T(4,128)}, f32[256,4,128]{0,2,1:T(8,128)S(1)}) fusion(bf16[256,512]{0,1:T(8,128)(2,1)S(1)} %copy.24, f32[256,4,128]{0,2,1:T(8,128)} %convolution_bitcast_fusion.9, f32[256,4,128]{0,2,1:T(8,128)S(1)} %convolution_bitcast_fusion.10, ...), kind=kOutput, calls=%fused_computation.49 | convolution fusion | flops 34599936 | bytes 2371588 | tf_op jit(solution)/shard_map/thi,hij->thj/dot_general | solution.py:68
  50.0 2.7 %convolution_bitcast_fusion = f32[2048,512]{0,1:T(8,128)} fusion(bf16[256,512]{0,1:T(8,128)(2,1)S(1)} %bitcast.165, bf16[1,256,2048]{2,1,0:T(8,128)(2,1)S(1)} %copy-done), kind=kOutput, calls=%fused_computation | convolution fusion | flops 536870912 | bytes 5505024 | tf_op jit(solution)/shard_map/dot_general | solution.py:114
  56.2 1.1 convolution_bitcast_fusion.5
  57.3 1.4 convolution_bitcast_fusion.1
  58.7 45.5 %reduce-scatter.2.cloned.1.call-done = f32[256,512]{0,1:T(8,128)} async-done(((f32[2048,512]{0,1:T(8,128)}), f32[256,512]{0,1:T(8,128)}) %reduce-scatter.2.cloned.1.call-update) | async-done | bytes 524304 | tf_op jit(solution)/shard_map/reduce_scatter | solution.py:113
  104.3 2.8 %convolution_bitcast_fusion.4 = f32[256,4,128]{0,2,1:T(8,128)} fusion(bf16[256,4,128]{2,1,0:T(4,128)(2,1)S(1)} %reshape_squeeze.9, f32[4,256,256]{1,2,0:T(8,128)} %copy-done.33, f32[4,256]{1,0:T(4,128)S(1)} %copy-done.26, f32[4,256]{1,0:T(4,128)S(1)} %copy-done.28, f32[4,256]{1,0:T(4,128)S(1)} %copy-done.24, pred[256,256]{0,1:T(8,128)(4,1)S(1)} %copy-done.17, ...), kind=kOutput, calls=%fused_computation.6 | convolution fusion | flops 69468160 | bytes 2109440 | tf_op jit(solution)/shard_map/hts,thd->shd/dot_general | solution.py:86
  107.0 1.4 fusion.55
  108.5 1.2 fusion.26
  109.7 1.5 collective-permute-start.4
  111.8 11.5 %collective-permute-done.4 = f32[2,4,128,128]{2,3,1,0:T(8,128)S(1)} collective-permute-done((f32[2,4,128,128]{2,3,1,0:T(8,128)S(1)}, f32[2,4,128,128]{2,3,1,0:T(8,128)S(1)}, u32[]{:S(2)}, u32[]{:S(2)}) %collective-permute-start.4) | collective-permute-done | bytes 524320 | tf_op jit(solution)/shard_map/ppermute | solution.py:10
  123.3 1.7 %fusion.20 = f32[1,4,128,128]{2,3,1,0:T(8,128)} fusion(f32[2,4,128,128]{2,3,1,0:T(8,128)S(1)} %collective-permute-done.4, f32[3,4,128,128]{2,3,1,0:T(8,128)} %collective-permute-done.3, f32[4,128,128]{2,1,0:T(8,128)S(1)} %convolution_multiply_fusion), kind=kLoop, calls=%fused_computation.55 | loop fusion | flops 131072 | bytes 1048576 | tf_op jit(solution)/shard_map/stack | solution.py:103
  125.0 1.5 collective-permute-start.5
  127.9 3.4 %fusion = bf16[1,256,2048]{2,1,0:T(8,128)(2,1)} fusion(bf16[256,512]{0,1:T(8,128)(2,1)S(1)} %bitcast.166, bf16[512,2048]{1,0:T(8,128)(2,1)} %all-gather.4.cloned.1.call-done), kind=kOutput, calls=%fused_computation.2 | convolution fusion | flops 537395200 | bytes 3407872 | tf_op jit(solution)/shard_map/dot_general | solution.py:73
  131.3 1.1 collective-permute-done.5
  135.6 15.9 %all-gather.6.cloned.1.call-done = f32[1024,512]{0,1:T(8,128)} async-done(((f32[256,512]{0,1:T(8,128)}), f32[1024,512]{0,1:T(8,128)}) %all-gather.6.cloned.1.call-update) | async-done | bytes 2097168 | tf_op jit(solution)/shard_map/all_gather | solution.py:121
  151.5 2.2 %reshape.193 = f32[4,256,512]{1,0,2:T(4,128)S(1)} reshape(f32[1024,512]{0,1:T(8,128)} %all-gather.6.cloned.1.call-done) | data formatting | bytes 4194304 | tf_op jit(solution)/shard_map/all_gather | solution.py:121
  153.7 2.1 %reduce_sum.69 = f32[256,512]{0,1:T(8,128)} reduce(f32[4,256,512]{1,0,2:T(4,128)S(1)} %reshape.193, f32[]{:T(128)} %constant.38.clone.1), dimensions={0}, to_apply=%region_7.8 | reduce | flops 393216 | bytes 2621444 | tf_op jit(solution)/shard_map/reduce_sum | solution.py:121
  (114 shorter events, 17.4 us)
Async XLA Ops:
  7.2 35.8 %copy-start = (bf16[1,256,2048]{2,1,0:T(8,128)(2,1)S(1)}, bf16[1,256,2048]{2,1,0:T(8,128)(2,1)}, u32[]{:S(2)}) copy-start(bf16[1,256,2048]{2,1,0:T(8,128)(2,1)} %param.11) | copy-start | bytes 3145732
  7.2 3.9 %copy-start.15 = (bf16[1,256,512]{2,1,0:T(8,128)(2,1)S(1)}, bf16[1,256,512]{2,1,0:T(8,128)(2,1)}, u32[]{:S(2)}) copy-start(bf16[1,256,512]{2,1,0:T(8,128)(2,1)} %param.6) | copy-start | bytes 786436
  7.2 4.0 %copy-start.20 = (f32[1,6,4,256]{3,2,1,0:T(4,128)S(1)}, f32[1,6,4,256]{3,2,1,0:T(4,128)}, u32[]{:S(2)}) copy-start(f32[1,6,4,256]{3,2,1,0:T(4,128)} %param.9) | copy-start | bytes 73732
  7.2 35.7 %all-gather.4.cloned.1.call-start = ((), (), s32[]{:S(2)}) async-start(), calls=%async_computation.1 | async-start | bytes 2359296 | tf_op jit(solution)/shard_map/all_gather | solution.py:72
  7.9 96.3 %reduce-scatter.2.cloned.1.call-start = ((), (), s32[]{:S(2)}) async-start(), calls=%async_computation.2 | async-start | bytes 4718592 | tf_op jit(solution)/shard_map/reduce_scatter | solution.py:113
  10.5 3.4 %collective-permute-start = (f32[4,128,128]{2,1,0:T(8,128)S(1)}, f32[4,128,128]{2,1,0:T(8,128)S(1)}, u32[]{:S(2)}, u32[]{:S(2)}) collective-permute-start(f32[4,128,128]{2,1,0:T(8,128)S(1)} %fusion.43), channel_id=1, source_target_pairs={{0,1},{1,0},{2,3},{3,2},{4,5},{5,4},{6,7},{7,6},{8,9},{9,8},{10,11... | collective-permute-start | bytes 786440 | tf_op jit(solution)/shard_map/ppermute | solution.py:10
  11.8 37.4 %copy-start.23 = (f32[4,256]{1,0:T(4,128)}, f32[4,256]{1,0:T(4,128)S(1)}, u32[]{:S(2)}) copy-start(f32[4,256]{1,0:T(4,128)S(1)} %get-tuple-element.23) | copy-start | bytes 12292
  11.8 37.4 %copy-start.25 = (f32[4,256]{1,0:T(4,128)}, f32[4,256]{1,0:T(4,128)S(1)}, u32[]{:S(2)}) copy-start(f32[4,256]{1,0:T(4,128)S(1)} %get-tuple-element.25) | copy-start | bytes 12292
  13.9 11.4 %collective-permute-start.1 = (f32[4,128,128]{2,1,0:T(8,128)S(1)}, f32[4,128,128]{2,1,0:T(8,128)S(1)}, u32[]{:S(2)}, u32[]{:S(2)}) collective-permute-start(f32[4,128,128]{2,1,0:T(8,128)S(1)} %add.91), channel_id=1, source_target_pairs={{0,2},{1,3},{2,0},{3,1},{4,6},{5,7},{6,4},{7,5},{8,10},{9,11},{10,... | collective-permute-start | bytes 786440 | tf_op jit(solution)/shard_map/ppermute | solution.py:10
  26.1 21.0 %collective-permute-start.2 = (f32[4,128,128]{2,1,0:T(8,128)}, f32[4,128,128]{2,1,0:T(8,128)S(1)}, u32[]{:S(2)}, u32[]{:S(2)}) collective-permute-start(f32[4,128,128]{2,1,0:T(8,128)} %add.93), channel_id=1, source_target_pairs={{0,4},{1,5},{2,6},{3,7},{4,0},{5,1},{6,2},{7,3},{8,12},{9,13},{10,... | collective-permute-start | bytes 786440 | tf_op jit(solution)/shard_map/ppermute | solution.py:10
  50.0 2.7 %copy-start.3 = (bf16[256,4,128]{0,2,1:T(8,128)(2,1)}, bf16[256,4,128]{0,2,1:T(8,128)(2,1)S(1)}, u32[]{:S(2)}) copy-start(bf16[256,4,128]{0,2,1:T(8,128)(2,1)S(1)} %fusion.7) | copy-start | bytes 786436
  52.7 2.8 %copy-start.17 = (pred[256,256]{0,1:T(8,128)(4,1)S(1)}, pred[256,256]{0,1:T(8,128)(4,1)}, u32[]{:S(2)}) copy-start(pred[256,256]{0,1:T(8,128)(4,1)} %get-tuple-element.31) | copy-start | bytes 196612
  52.7 2.7 %copy-start.19 = (pred[256,256]{0,1:T(8,128)(4,1)S(1)}, pred[256,256]{0,1:T(8,128)(4,1)}, u32[]{:S(2)}) copy-start(pred[256,256]{0,1:T(8,128)(4,1)} %iota_compare_fusion) | copy-start | bytes 196612
  52.7 98.8 %all-gather.6.cloned.1.call-start = ((), (), s32[]{:S(2)}) async-start(), calls=%async_computation.3 | async-start | bytes 2621440 | tf_op jit(solution)/shard_map/all_gather | solution.py:121
  55.2 53.3 %collective-permute-start.3 = (f32[3,4,128,128]{2,3,1,0:T(8,128)}, f32[3,4,128,128]{2,3,1,0:T(8,128)}, u32[]{:S(2)}, u32[]{:S(2)}) collective-permute-start(f32[3,4,128,128]{2,3,1,0:T(8,128)} %pad_maximum_fusion), channel_id=1, source_target_pairs={{0,1},{1,0},{2,3},{3,2},{4,5},{5,4},{6,7},{7,6},{8,9},{9,8},{10,11... | collective-permute-start | bytes 2359304 | tf_op jit(solution)/shard_map/ppermute | solution.py:10
  104.3 2.8 %copy-start.9 = (f32[4,256,256]{1,2,0:T(8,128)S(1)}, f32[4,256,256]{1,2,0:T(8,128)}, u32[]{:S(2)}) copy-start(f32[4,256,256]{1,2,0:T(8,128)} %fusion.31) | copy-start | bytes 3145732
  104.3 4.2 %copy-start.32 = (f32[6,4,256]{2,1,0:T(4,128)}, f32[6,4,256]{2,1,0:T(4,128)S(1)}, u32[]{:S(2)}) copy-start(f32[6,4,256]{2,1,0:T(4,128)S(1)} %constant_dynamic-update-slice_fusion.1) | copy-start | bytes 73732
  108.5 3.0 %copy-start.1 = (f32[256,4,128]{0,2,1:T(8,128)S(1)}, f32[256,4,128]{0,2,1:T(8,128)}, u32[]{:S(2)}) copy-start(f32[256,4,128]{0,2,1:T(8,128)} %convolution_bitcast_fusion.5) | copy-start | bytes 1572868
  108.5 3.0 %copy-start.14 = (f32[256,4,128]{0,2,1:T(8,128)S(1)}, f32[256,4,128]{0,2,1:T(8,128)}, u32[]{:S(2)}) copy-start(f32[256,4,128]{0,2,1:T(8,128)} %convolution_bitcast_fusion.1) | copy-start | bytes 1572868
  109.7 13.6 %collective-permute-start.4 = (f32[2,4,128,128]{2,3,1,0:T(8,128)S(1)}, f32[2,4,128,128]{2,3,1,0:T(8,128)S(1)}, u32[]{:S(2)}, u32[]{:S(2)}) collective-permute-start(f32[2,4,128,128]{2,3,1,0:T(8,128)S(1)} %pad_maximum_fusion.1), channel_id=1, source_target_pairs={{0,2},{1,3},{2,0},{3,1},{4,6},{5,7},{6,4},{7,5},{8,10},{9,11},{10,... | collective-permute-start | bytes 1572872 | tf_op jit(solution)/shard_map/ppermute | solution.py:10
  111.5 16.4 %copy-start.4 = (bf16[256,4,128]{0,2,1:T(8,128)(2,1)S(1)}, bf16[256,4,128]{0,2,1:T(8,128)(2,1)}, u32[]{:S(2)}) copy-start(bf16[256,4,128]{0,2,1:T(8,128)(2,1)} %copy-done.3) | copy-start | bytes 786436
  125.0 7.4 %collective-permute-start.5 = (f32[1,4,128,128]{2,3,1,0:T(8,128)}, f32[1,4,128,128]{2,3,1,0:T(8,128)S(1)}, u32[]{:S(2)}, u32[]{:S(2)}) collective-permute-start(f32[1,4,128,128]{2,3,1,0:T(8,128)} %fusion.20), channel_id=1, source_target_pairs={{0,4},{1,5},{2,6},{3,7},{4,0},{5,1},{6,2},{7,3},{8,12},{9,13},{10,... | collective-permute-start | bytes 786440 | tf_op jit(solution)/shard_map/ppermute | solution.py:10
  127.9 5.5 %copy-start.13 = (f32[256,4,128]{0,2,1:T(8,128)S(1)}, f32[256,4,128]{0,2,1:T(8,128)}, u32[]{:S(2)}) copy-start(f32[256,4,128]{0,2,1:T(8,128)} %convolution_bitcast_fusion.4) | copy-start | bytes 1572868
  131.3 3.2 %copy-start.12 = (f32[4,128,256]{2,1,0:T(8,128)S(1)}, f32[4,128,256]{2,1,0:T(8,128)}, u32[]{:S(2)}) copy-start(f32[4,128,256]{2,1,0:T(8,128)} %fusion.55) | copy-start | bytes 1572868
  (19 other events, 37.3 us)
Sparse Core Ops, SparseCore 0:
  9.9 32.9 all-gather.3
  52.8 51.3 reduce-scatter.1
  105.8 45.6 all-gather.5
